TPU v7x, 32 devices: a whole 2x2x4 slice. The times are simulated.
32 devices in a mesh: sta: 8 (over z, core), cell: 4 (over y, x).
Axes of the slice: x: 2, y: 2, z: 4, core: 2. Of those that a mesh axis runs over, the one named last changes fastest.
Arguments:
- station_xyz: float32 [3, 2048], P(None, 'sta'), may hold values from 0 to 1, as said below
- cell_xyz: float32 [3, 131072], P(None, 'cell'), may hold values from -0.6 to 1, as said below
- cell_weight: float32 [131072], P('cell'), may hold values from 0.3 to 3
- data: float32 [2048], P(('sta', 'cell')), may hold values from -6 to 6
- model_start: float32 [131072], P(('cell', 'sta')), may hold values from -6 to 6
Outputs:
- model_next: float32 [131072], P(('cell', 'sta'))
- residual_next: float32 [2048], P(('sta', 'cell'))
- search_next: float32 [131072], P(('cell', 'sta'))
Inputs may be any that keep to these rules, and one draw needn't show every extreme that they name: `station_xyz`: rows 0 and 1 lie in [0, 1), row 2 in [0, 0.05]. `cell_xyz`: rows 0 and 1 lie in [0, 1), row 2 in [-0.6, -0.02].
All inputs are finite; a program needn't handle non-finite values.
Results may differ from a plain program's by a relative error of at most 0.0003.
Values sent between devices are 32-bit elements; how exact they have to be, the bound alone decides.
A program may use at most 64 MiB of HBM per device.

v0:
```python
import functools
import math

import jax
import jax.numpy as jnp
from jax import lax
from jax.experimental import pallas as pl
from jax.experimental.pallas import tpu as pltpu
from jax.sharding import PartitionSpec as P

SOFT = 0.0001
LANES = 128
FEATURES = 96
MESH = pl.DeviceIdType.MESH
F32 = jnp.float32


def bf_pieces(x):
    a = x.astype(jnp.bfloat16).astype(F32)
    b = (x - a).astype(jnp.bfloat16).astype(F32)
    c = (x - a - b).astype(jnp.bfloat16).astype(F32)
    return a, b, c


def coordinate_pieces(x):
    row = lax.broadcasted_iota(jnp.int32, x.shape, 0)
    shift = jnp.where(row < 2, -0.5, jnp.where(row == 2, 0.275, 0.0))
    x = jnp.where(row < 3, x + shift, 0.0)
    h = jnp.round(x * 256.0) * (1.0 / 256.0)
    rest = x - h
    m = jnp.round(rest * 65536.0) * (1.0 / 65536.0)
    l = (rest - m).astype(jnp.bfloat16).astype(F32)
    return row, h, m, l


def norm_pieces(h, m, l, soft):
    a = jnp.sum(h * h, axis=0, keepdims=True)
    ml = m + l
    b = jnp.sum(2.0 * h * ml + ml * ml, axis=0, keepdims=True) + soft
    a1 = jnp.round(a * 256.0) * (1.0 / 256.0)
    return (a1, a - a1) + bf_pieces(b)


def rows_of(row, items):
    out = jnp.zeros(row.shape, F32)
    for at, item in items.items():
        out = jnp.where(row == at, item, out)
    return out


def cell_features(x, u, w):
    row, h, m, l = coordinate_pieces(x)
    a1, a2, b1, b2, b3 = norm_pieces(h, m, l, 0.0)
    first = h + rows_of(row, {3: 1.0, 4: 1.0, 5: a1, 6: a2})
    norms = rows_of(row, {0: 1.0, 1: 1.0, 2: 1.0, 3: b1, 4: b2, 5: b3})
    u1, u2, u3 = bf_pieces(u)
    w1, w2, w3 = bf_pieces(w)
    vectors = rows_of(row, {0: u1, 1: u2, 2: u3, 3: w1, 4: w2, 5: w3})
    zero = jnp.zeros_like(x)
    return jnp.concatenate([first, h, h, m, m, m, l, l, l, norms, vectors, zero], axis=0)


def station_features(x):
    row, h, m, l = coordinate_pieces(x)
    a1, a2, b1, b2, b3 = norm_pieces(h, m, l, SOFT)
    first = -2.0 * h + rows_of(row, {3: a1, 4: a2, 5: 1.0, 6: 1.0})
    norms = rows_of(row, {0: b1, 1: b2, 2: b3, 3: 1.0, 4: 1.0, 5: 1.0})
    h, m, l = -2.0 * h, -2.0 * m, -2.0 * l
    zero = jnp.zeros_like(x)
    return jnp.concatenate([first, m, l, h, m, l, h, m, l, norms, zero, zero], axis=0)


def spread_matrix():
    row = lax.broadcasted_iota(jnp.int32, (FEATURES, 3 * LANES), 0)
    col = lax.broadcasted_iota(jnp.int32, (FEATURES, 3 * LANES), 1)
    z = (row == 2) | (row == 26) | (row == 50)
    u = (row >= 80) & (row < 83)
    w = (row >= 83) & (row < 86)
    pick = ((col < LANES) & z) | ((col >= LANES) & (col < 2 * LANES) & u) | ((col >= 2 * LANES) & w)
    return jnp.where(pick, 1.0, 0.0).astype(jnp.bfloat16)


def kernel(sizes, st_ref, cell_ref, w_ref, m_ref, data_ref, model_ref, res_ref, search_ref,
           kmat, lhs, czb, ub, wb, gb, grow, st_all, szb, rbc, rs1, rs2, ag1, ag2, gn, out1, out2,
           send_sem, recv_sem):
    n_sta, n_cell, cells, width, piece, scale, mb = sizes
    n = n_sta * n_cell
    groups = cells // 8
    blocks = cells // LANES
    per_tile = LANES // piece
    tiles = width // LANES
    my_sta, my_cell = lax.axis_index("sta"), lax.axis_index("cell")
    me = my_sta * n_cell + my_cell

    def peer(k):
        flat = lax.rem(me + k, n)
        return (flat // n_cell, lax.rem(flat, n_cell))

    barrier = pltpu.get_barrier_semaphore()

    def greet(k, c):
        pl.semaphore_signal(barrier, inc=1, device_id=peer(k), device_id_type=MESH)
        return c

    lax.fori_loop(1, n, greet, 0)

    lane = lax.broadcasted_iota(jnp.int32, (1, LANES), 1)
    own = lane < piece

    spread = spread_matrix()

    def prepare(b, c):
        at = pl.multiple_of(b * LANES, LANES)
        cols = pl.ds(at, LANES)
        w = w_ref[:, cols] * scale
        feats = cell_features(cell_ref[:, cols], w * m_ref[:, cols], w)
        rows = jnp.transpose(feats).astype(jnp.bfloat16)
        lhs[cols, :] = rows
        wide = jnp.dot(rows, spread, preferred_element_type=F32)
        gs = pl.ds(b * (LANES // 8), LANES // 8)
        czb[gs] = wide[:, :LANES].reshape(LANES // 8, 8, LANES) - 0.275
        ub[gs] = wide[:, LANES:2 * LANES].reshape(LANES // 8, 8, LANES)
        wb[gs] = wide[:, 2 * LANES:].reshape(LANES // 8, 8, LANES)
        return c

    lax.fori_loop(0, blocks, prepare, 0)

    st_all[my_sta] = st_ref[...]
    pl.semaphore_wait(barrier, n - 1)

    def send_stations(k, c):
        pltpu.make_async_remote_copy(
            src_ref=st_ref, dst_ref=st_all.at[my_sta], send_sem=send_sem.at[0], recv_sem=recv_sem.at[0],
            device_id=(lax.rem(my_sta + k, n_sta), my_cell), device_id_type=MESH).start()
        return c

    lax.fori_loop(1, n_sta, send_stations, 0)

    def bulk_wait(buf, count, sems, which):
        part = buf.at[pl.ds(0, count)]
        pltpu.make_async_copy(part, part, sems.at[which]).wait()

    def send_block(out, rs, which, k, s, rows, fill):
        for c in range(n_cell):
            tile, q = (c * piece) // LANES, c % per_tile
            value = rows[tile]
            if q:
                value = pltpu.roll(value, LANES - q * piece, 1)
            if fill is not None:
                value = jnp.where(own, value, fill)
            out[s * n_cell + c] = value
        for c in range(n_cell):
            target = s * n_cell + c

            @pl.when(target != me)
            def _():
                pltpu.make_async_remote_copy(
                    src_ref=out.at[target], dst_ref=rs.at[me], send_sem=send_sem.at[which],
                    recv_sem=recv_sem.at[which], device_id=(s, c), device_id_type=MESH).start()

            @pl.when(target == me)
            def _():
                rs[me] = out[target]

    def broadcast(buf, which):
        def one(k, c):
            pltpu.make_async_remote_copy(
                src_ref=buf.at[me], dst_ref=buf.at[me], send_sem=send_sem.at[which],
                recv_sem=recv_sem.at[which], device_id=peer(k), device_id_type=MESH).start()
            return c
        lax.fori_loop(1, n, one, 0)

    def total(buf):
        return jnp.sum(buf[...], axis=0)

    def sta_block(k, c):
        s = lax.rem(my_sta + k, n_sta)

        @pl.when(k == 1)
        def _():
            bulk_wait(st_all, n_sta - 1, recv_sem, 0)

        x = st_all[s]
        rhs = station_features(x).astype(jnp.bfloat16)
        sz = jnp.broadcast_to(x[2:3, :], (8, width))

        def block(b, accs):
            at = pl.multiple_of(b * mb, mb)
            r2 = jnp.dot(lhs[pl.ds(at, mb), :], rhs, preferred_element_type=F32)
            gs = pl.ds(b * (mb // 8), mb // 8)
            cz, u = czb[gs], ub[gs]
            out = []
            for t in range(tiles):
                part = r2[:, t * LANES:(t + 1) * LANES].reshape(mb // 8, 8, LANES)
                inv = lax.rsqrt(part)
                dz = sz[None, :, t * LANES:(t + 1) * LANES] - cz
                value = (dz * inv) * (inv * inv)
                kmat[s, gs, :, t * LANES:(t + 1) * LANES] = value
                out.append(accs[t] + jnp.sum(value * u, axis=0))
            return tuple(out)

        accs = lax.fori_loop(0, cells // mb, block, tuple(jnp.zeros((8, LANES), F32) for _ in range(tiles)))
        rows = [jnp.sum(a, axis=0, keepdims=True) for a in accs]
        send_block(out1, rs1, 1, k, s, rows, None)
        return c

    lax.fori_loop(0, n_sta, sta_block, 0)
    bulk_wait(rs1, n - 1, recv_sem, 1)
    ag1[me] = data_ref[...] - total(rs1)
    broadcast(ag1, 2)

    def spread_rows(buf, dst):
        def one(s, c):
            for t in range(tiles):
                row = jnp.zeros((1, LANES), F32)
                for q in range(per_tile):
                    value = jnp.where(own, buf[s * n_cell + t * per_tile + q], 0.0)
                    if q:
                        value = pltpu.roll(value, q * piece, 1)
                    row = row + value
                dst[s, :, t * LANES:(t + 1) * LANES] = jnp.broadcast_to(row, (8, LANES))
            return c
        lax.fori_loop(0, n_sta, one, 0)

    bulk_wait(ag1, n - 1, recv_sem, 2)
    spread_rows(ag1, rbc)

    step = 8

    def backward(b, sq):
        gs = pl.ds(b * step, step)
        acc = jnp.zeros((step, 8, LANES), F32)
        for s in range(n_sta):
            for t in range(tiles):
                cols = slice(t * LANES, (t + 1) * LANES)
                acc = acc + kmat[s, gs, :, cols] * rbc[s, :, cols][None]
        g = jnp.sum(acc, axis=2, keepdims=True) * wb[gs]
        gb[gs] = g
        return sq + jnp.sum(g * g, axis=0)

    sq = lax.fori_loop(0, groups // step, backward, jnp.zeros((8, LANES), F32))
    gamma_part = jnp.sum(sq, axis=0, keepdims=True)

    def weigh(b, c):
        gs = pl.ds(b * 16, 16)
        ub[gs] = gb[gs] * wb[gs]
        return c

    lax.fori_loop(0, groups // 16, weigh, 0)

    together = 4

    def image_block(k, c):
        ss = [lax.rem(my_sta + k * together + i, n_sta) for i in range(together)]

        def block(b, accs):
            gs = pl.ds(b * 8, 8)
            u = ub[gs]
            out = []
            for i in range(together):
                for t in range(tiles):
                    value = kmat[ss[i], gs, :, t * LANES:(t + 1) * LANES] * u
                    out.append(accs[i * tiles + t] + jnp.sum(value, axis=0))
            return tuple(out)

        accs = lax.fori_loop(0, groups // 8, block,
                             tuple(jnp.zeros((8, LANES), F32) for _ in range(together * tiles)))
        for i in range(together):
            rows = [jnp.sum(a, axis=0, keepdims=True) for a in accs[i * tiles:(i + 1) * tiles]]
            send_block(out2, rs2, 3, k, ss[i], rows, gamma_part)
        return c

    lax.fori_loop(0, n_sta // together, image_block, 0)
    eye = (lax.broadcasted_iota(jnp.int32, (16, 8, LANES), 0) * 8
           + lax.broadcasted_iota(jnp.int32, (16, 8, LANES), 1)
           == lax.broadcasted_iota(jnp.int32, (16, 8, LANES), 2))

    def as_row(b):
        block = jnp.where(eye, gb[pl.ds(b * 16, 16)], 0.0)
        return jnp.sum(jnp.sum(block, axis=0), axis=0, keepdims=True)

    bulk_wait(rs2, n - 1, recv_sem, 3)
    ag2[me] = total(rs2)
    broadcast(ag2, 4)

    def keep_row(b, c):
        grow[:, pl.ds(pl.multiple_of(b * LANES, LANES), LANES)] = as_row(b)
        return c

    lax.fori_loop(0, blocks, keep_row, 0)
    bulk_wait(ag2, n - 1, recv_sem, 4)
    images = jnp.where(own[None], ag2[...], 0.0)
    delta = jnp.sum(jnp.sum(images * images, axis=0), axis=1, keepdims=True)
    mine = ag2[me]
    gamma = jnp.sum(jnp.where(lane == piece, mine, 0.0), axis=1, keepdims=True)
    alpha = gamma / delta
    res_ref[...] = ag1[me] - alpha * mine
    ag1_next = ag1[...] - alpha[None] * ag2[...]
    rs1[...] = ag1_next
    spread_rows(rs1, rbc)

    sq = lax.fori_loop(0, groups // step, backward, jnp.zeros((8, LANES), F32))
    gn[me] = jnp.sum(sq, axis=0, keepdims=True)
    broadcast(gn, 5)

    def next_row(b, c):
        cols = pl.ds(pl.multiple_of(b * LANES, LANES), LANES)
        search_ref[:, cols] = as_row(b)
        model_ref[:, cols] = m_ref[:, cols] + alpha * grow[:, cols]
        return c

    lax.fori_loop(0, blocks, next_row, 0)
    bulk_wait(gn, n - 1, recv_sem, 5)
    beta = total(gn)[:, :1] / gamma
    search_ref[...] = search_ref[...] + beta * grow[...]

    bulk_wait(st_all, n_sta - 1, send_sem, 0)
    for which, buf in ((1, rs1), (2, ag1), (3, rs2), (4, ag2), (5, gn)):
        bulk_wait(buf, n - 1, send_sem, which)


def per_device(station_xyz, cell_xyz, cell_weight, data, model_start):
    n_sta, n_cell = lax.axis_size("sta"), lax.axis_size("cell")
    n = n_sta * n_cell
    width = station_xyz.shape[1]
    cells = model_start.shape[0]
    piece = data.shape[0]
    scale = 1.0 / math.sqrt(width * n_sta * cells * n)
    at = lax.axis_index("sta") * cells
    own_cells = jnp.pad(lax.dynamic_slice_in_dim(cell_xyz, at, cells, 1), ((0, 5), (0, 0)))
    own_weight = lax.dynamic_slice_in_dim(cell_weight, at, cells, 0).reshape(1, cells)
    stations = jnp.pad(station_xyz, ((0, 5), (0, 0)))
    data_row = jnp.pad(data, (0, LANES - piece)).reshape(1, LANES)
    groups = cells // 8
    mb = min(1024, cells)
    sizes = (n_sta, n_cell, cells, width, piece, scale, mb)
    vmem = pl.BlockSpec(memory_space=pltpu.VMEM)
    wide = pltpu.VMEM((groups, 8, LANES), F32)
    message = pltpu.VMEM((n, 1, LANES), F32)
    model_next, residual, search = pl.pallas_call(
        functools.partial(kernel, sizes),
        out_shape=(jax.ShapeDtypeStruct((1, cells), F32), jax.ShapeDtypeStruct((1, LANES), F32),
                   jax.ShapeDtypeStruct((1, cells), F32)),
        in_specs=[vmem] * 5,
        out_specs=(vmem, vmem, vmem),
        scratch_shapes=[
            pltpu.VMEM((n_sta, groups, 8, width), F32),
            pltpu.VMEM((cells, FEATURES), jnp.bfloat16),
            wide, wide, wide, wide,
            pltpu.VMEM((1, cells), F32),
            pltpu.VMEM((n_sta, 8, width), F32),
            pltpu.VMEM((n_sta, 8, width), F32),
            pltpu.VMEM((n_sta, 8, width), F32),
            message, message, message, message, message, message, message,
            pltpu.SemaphoreType.DMA((6,)),
            pltpu.SemaphoreType.DMA((6,)),
        ],
        compiler_params=pltpu.CompilerParams(
            collective_id=0, has_side_effects=True, vmem_limit_bytes=60 * 1024 * 1024),
    )(stations, own_cells, own_weight, model_start.reshape(1, cells), data_row)
    return (model_next.reshape(cells), residual[0, :piece], search.reshape(cells))


def solution(mesh):
    placed = (P(None, "sta"), P(None, "cell"), P("cell"), P(("sta", "cell")), P(("cell", "sta")))
    return jax.shard_map(
        per_device,
        mesh=mesh,
        in_specs=placed,
        out_specs=(P(("cell", "sta")), P(("sta", "cell")), P(("cell", "sta"))),
        check_vma=False,
    )
```

profile of v0, /device:TPU:0, one launch (start us, length us, event | category | flops | bytes accessed | tf_op | source)
XLA Modules:
  0.0 79.5 jit_solution(1494126009245211690)
XLA Ops:
  0.6 0.0 copy-start
  0.7 1.0 %copy-done = f32[3,32768]{1,0:T(4,128)S(1)} copy-done((f32[3,32768]{1,0:T(4,128)S(1)}, f32[3,32768]{1,0:T(4,128)}, u32[]{:S(2)}) %copy-start) | copy-done | bytes 393240
  1.7 0.7 pad.13.cell_ref
  2.4 0.0 copy-start.2
  2.4 1.3 %dynamic_slice.7 = f32[4096]{0:T(1024)} dynamic-slice(f32[32768]{0:T(1024)} %param.7, s32[]{:T(128)S(6)} %select_n.4), dynamic_slice_sizes={4096} | dynamic-slice | bytes 32772 | tf_op jit(solution)/shard_map/dynamic_slice | solution.py:331
  3.7 0.0 copy-done.2
  3.7 0.0 copy-start.3
  3.7 0.6 pad.12.st_ref
  4.3 0.1 copy-done.3
  4.4 0.5 pad_bitcast_fusion.data_ref
  4.9 71.5 %shard_map.76 = (f32[1,4096]{1,0:T(1,128)}, f32[1,128]{1,0:T(1,128)}, f32[1,4096]{1,0:T(1,128)}) custom-call(f32[8,256]{1,0:T(8,128)} %pad.12.st_ref, f32[8,4096]{1,0:T(8,128)} %pad.13.cell_ref, f32[1,4096]{1,0:T(1,128)} %bitcast.8, f32[1,4096]{1,0:T(1,128)} %bitcast.11, f32[1,128]{1,0:T(1,128)} %pad_bitcast_fusion.data_ref), custom_call_target="tpu_custom_call" | custom-call | tf_op jit(solution)/shard_map/pallas_call | solution.py:340
  76.4 0.0 copy-start.4
  76.4 0.7 copy-done.4
  77.1 0.5 slice_bitcast_fusion
  77.6 0.0 copy-start.1
  77.6 1.3 %copy.10 = f32[4096]{0:T(1024)} copy(f32[4096]{0:T(1024)} %bitcast.10) | data formatting | bytes 32768
  78.9 0.0 copy-done.1
  78.9 0.6 copy.11
  (1 shorter events, 0.0 us)
Async XLA Ops:
  0.6 1.0 %copy-start = (f32[3,32768]{1,0:T(4,128)S(1)}, f32[3,32768]{1,0:T(4,128)}, u32[]{:S(2)}) copy-start(f32[3,32768]{1,0:T(4,128)} %param.6) | copy-start | bytes 1179652
  2.4 1.3 %copy-start.2 = (f32[3,256]{1,0:T(4,128)S(1)}, f32[3,256]{1,0:T(4,128)}, u32[]{:S(2)}) copy-start(f32[3,256]{1,0:T(4,128)} %param.5) | copy-start | bytes 9220
  3.7 0.7 copy-start.3
  76.4 0.7 copy-start.4
  77.6 1.3 %copy-start.1 = (f32[1,4096]{1,0:T(1,128)S(1)}, f32[1,4096]{1,0:T(1,128)}, u32[]{:S(2)}) copy-start(f32[1,4096]{1,0:T(1,128)} %get-tuple-element.8) | copy-start | bytes 49156
where the time goes:
time: 79.8 us; the launch traced here: 79.5 us
  Pallas kernels  71.5 us (90%)
  local copies, waits for them, and re-layouts  7.33 us (9%)
    pallas_call x1, Pallas kernels, per_device(): pl.pallas_call(functools.partial(kernel, sizes), out_shape=(jax.ShapeDtyp...  71.5 us
    unnamed x12, local copies, waits for them, and re-layouts  3.7 us

commit v1 on v0

--- a/solution.py
+++ b/solution.py
@@ -81,7 +81,7 @@
 
 
 def kernel(sizes, st_ref, cell_ref, w_ref, m_ref, data_ref, model_ref, res_ref, search_ref,
-           kmat, lhs, czb, ub, wb, gb, grow, st_all, szb, rbc, rs1, rs2, ag1, ag2, gn, out1, out2,
+           kmat, lhs, czb, ub, wb, gb, grow, st_all, szb, rbc, rs1, rs2, ag1, ag2, gm, gn, out1, out2,
            send_sem, recv_sem):
     n_sta, n_cell, cells, width, piece, scale, mb = sizes
     n = n_sta * n_cell
@@ -123,7 +123,7 @@
         wb[gs] = wide[:, 2 * LANES:].reshape(LANES // 8, 8, LANES)
         return c
 
-    lax.fori_loop(0, blocks, prepare, 0)
+    lax.fori_loop(0, blocks, prepare, 0, unroll=4)
 
     st_all[my_sta] = st_ref[...]
     pl.semaphore_wait(barrier, n - 1)
@@ -140,27 +140,28 @@
         part = buf.at[pl.ds(0, count)]
         pltpu.make_async_copy(part, part, sems.at[which]).wait()
 
-    def send_block(out, rs, which, k, s, rows, fill):
+    def send_block(out, rs, which, s, rows):
+        row = jnp.concatenate(rows, axis=1)
+        out[s] = row
+        rs[me, s] = row
+
+        def one(k, c):
+            pltpu.make_async_remote_copy(
+                src_ref=out.at[s], dst_ref=rs.at[me, s], send_sem=send_sem.at[which],
+                recv_sem=recv_sem.at[which], device_id=peer(k), device_id_type=MESH).start()
+            return c
+
+        lax.fori_loop(1, n, one, 0)
+
+    def own_piece(row):
+        out = jnp.zeros((1, LANES), F32)
         for c in range(n_cell):
             tile, q = (c * piece) // LANES, c % per_tile
-            value = rows[tile]
+            value = row[:, tile * LANES:(tile + 1) * LANES]
             if q:
                 value = pltpu.roll(value, LANES - q * piece, 1)
-            if fill is not None:
-                value = jnp.where(own, value, fill)
-            out[s * n_cell + c] = value
-        for c in range(n_cell):
-            target = s * n_cell + c
-
-            @pl.when(target != me)
-            def _():
-                pltpu.make_async_remote_copy(
-                    src_ref=out.at[target], dst_ref=rs.at[me], send_sem=send_sem.at[which],
-                    recv_sem=recv_sem.at[which], device_id=(s, c), device_id_type=MESH).start()
-
-            @pl.when(target == me)
-            def _():
-                rs[me] = out[target]
+            out = jnp.where(my_cell == c, value, out)
+        return out
 
     def broadcast(buf, which):
         def one(k, c):
@@ -201,52 +202,61 @@
 
         accs = lax.fori_loop(0, cells // mb, block, tuple(jnp.zeros((8, LANES), F32) for _ in range(tiles)))
         rows = [jnp.sum(a, axis=0, keepdims=True) for a in accs]
-        send_block(out1, rs1, 1, k, s, rows, None)
+        first = jnp.where(k == 0, 1.0, 0.0)
+        for q in range(n_cell):
+            tile, at = (q * piece) // LANES, q % per_tile
+            value = jnp.where(own, data_ref[...], 0.0) * jnp.where(my_cell == q, first, 0.0)
+            if at:
+                value = pltpu.roll(value, at * piece, 1)
+            rows[tile] = rows[tile] - value
+        send_block(out1, rs1, 1, s, rows)
         return c
 
     lax.fori_loop(0, n_sta, sta_block, 0)
     bulk_wait(rs1, n - 1, recv_sem, 1)
-    ag1[me] = data_ref[...] - total(rs1)
-    broadcast(ag1, 2)
-
-    def spread_rows(buf, dst):
-        def one(s, c):
-            for t in range(tiles):
-                row = jnp.zeros((1, LANES), F32)
-                for q in range(per_tile):
-                    value = jnp.where(own, buf[s * n_cell + t * per_tile + q], 0.0)
-                    if q:
-                        value = pltpu.roll(value, q * piece, 1)
-                    row = row + value
-                dst[s, :, t * LANES:(t + 1) * LANES] = jnp.broadcast_to(row, (8, LANES))
-            return c
-        lax.fori_loop(0, n_sta, one, 0)
-
-    bulk_wait(ag1, n - 1, recv_sem, 2)
-    spread_rows(ag1, rbc)
+
+    def residual(s, c):
+        row = -jnp.sum(rs1[:, s], axis=0)
+        ag1[s] = row
+        rbc[s] = jnp.broadcast_to(row, (8, width))
+        return c
+
+    lax.fori_loop(0, n_sta, residual, 0)
 
     step = 8
 
-    def backward(b, sq):
+    def backward(b, c):
         gs = pl.ds(b * step, step)
         acc = jnp.zeros((step, 8, LANES), F32)
         for s in range(n_sta):
             for t in range(tiles):
                 cols = slice(t * LANES, (t + 1) * LANES)
                 acc = acc + kmat[s, gs, :, cols] * rbc[s, :, cols][None]
-        g = jnp.sum(acc, axis=2, keepdims=True) * wb[gs]
-        gb[gs] = g
-        return sq + jnp.sum(g * g, axis=0)
-
-    sq = lax.fori_loop(0, groups // step, backward, jnp.zeros((8, LANES), F32))
-    gamma_part = jnp.sum(sq, axis=0, keepdims=True)
-
-    def weigh(b, c):
+        gb[gs] = acc
+        return c
+
+    ones = jnp.ones((3 * LANES, LANES), jnp.bfloat16)
+    eye = (lax.broadcasted_iota(jnp.int32, (16, 8, LANES), 0) * 8
+           + lax.broadcasted_iota(jnp.int32, (16, 8, LANES), 1)
+           == lax.broadcasted_iota(jnp.int32, (16, 8, LANES), 2))
+
+    def finish(dst, b, sq):
         gs = pl.ds(b * 16, 16)
-        ub[gs] = gb[gs] * wb[gs]
-        return c
-
-    lax.fori_loop(0, groups // 16, weigh, 0)
+        parts = jnp.concatenate(bf_pieces(gb[gs].reshape(LANES, LANES)), axis=1).astype(jnp.bfloat16)
+        w = wb[gs]
+        g = jnp.dot(parts, ones, preferred_element_type=F32).reshape(16, 8, LANES) * w
+        ub[gs] = g * w
+        row = jnp.sum(jnp.sum(jnp.where(eye, g, 0.0), axis=0), axis=0, keepdims=True)
+        dst[:, pl.ds(pl.multiple_of(b * LANES, LANES), LANES)] = row
+        return sq + row * row
+
+    def gradient(dst):
+        lax.fori_loop(0, groups // step, backward, 0)
+        sq = lax.fori_loop(0, blocks, functools.partial(finish, dst), jnp.zeros((1, LANES), F32), unroll=4)
+        return jnp.broadcast_to(jnp.sum(sq, axis=1, keepdims=True), (1, LANES))
+
+    gm[me] = gradient(grow)
+    broadcast(gm, 2)
 
     together = 4
 
@@ -267,55 +277,38 @@
                              tuple(jnp.zeros((8, LANES), F32) for _ in range(together * tiles)))
         for i in range(together):
             rows = [jnp.sum(a, axis=0, keepdims=True) for a in accs[i * tiles:(i + 1) * tiles]]
-            send_block(out2, rs2, 3, k, ss[i], rows, gamma_part)
+            send_block(out2, rs2, 3, ss[i], rows)
         return c
 
     lax.fori_loop(0, n_sta // together, image_block, 0)
-    eye = (lax.broadcasted_iota(jnp.int32, (16, 8, LANES), 0) * 8
-           + lax.broadcasted_iota(jnp.int32, (16, 8, LANES), 1)
-           == lax.broadcasted_iota(jnp.int32, (16, 8, LANES), 2))
-
-    def as_row(b):
-        block = jnp.where(eye, gb[pl.ds(b * 16, 16)], 0.0)
-        return jnp.sum(jnp.sum(block, axis=0), axis=0, keepdims=True)
-
+    bulk_wait(gm, n - 1, recv_sem, 2)
+    gamma = total(gm)[:, :1]
     bulk_wait(rs2, n - 1, recv_sem, 3)
-    ag2[me] = total(rs2)
-    broadcast(ag2, 4)
-
-    def keep_row(b, c):
-        grow[:, pl.ds(pl.multiple_of(b * LANES, LANES), LANES)] = as_row(b)
-        return c
-
-    lax.fori_loop(0, blocks, keep_row, 0)
-    bulk_wait(ag2, n - 1, recv_sem, 4)
-    images = jnp.where(own[None], ag2[...], 0.0)
-    delta = jnp.sum(jnp.sum(images * images, axis=0), axis=1, keepdims=True)
-    mine = ag2[me]
-    gamma = jnp.sum(jnp.where(lane == piece, mine, 0.0), axis=1, keepdims=True)
-    alpha = gamma / delta
-    res_ref[...] = ag1[me] - alpha * mine
-    ag1_next = ag1[...] - alpha[None] * ag2[...]
-    rs1[...] = ag1_next
-    spread_rows(rs1, rbc)
-
-    sq = lax.fori_loop(0, groups // step, backward, jnp.zeros((8, LANES), F32))
-    gn[me] = jnp.sum(sq, axis=0, keepdims=True)
+
+    def image_sum(s, sq):
+        row = jnp.sum(rs2[:, s], axis=0)
+        ag2[s] = row
+        return sq + row * row
+
+    sq = lax.fori_loop(0, n_sta, image_sum, jnp.zeros((1, width), F32))
+    alpha = gamma / jnp.sum(sq, axis=1, keepdims=True)
+
+    def residual_next(s, c):
+        rbc[s] = jnp.broadcast_to(ag1[s] - alpha * ag2[s], (8, width))
+        return c
+
+    lax.fori_loop(0, n_sta, residual_next, 0)
+    res_ref[...] = own_piece(ag1[my_sta] - alpha * ag2[my_sta])
+
+    gn[me] = gradient(search_ref)
     broadcast(gn, 5)
-
-    def next_row(b, c):
-        cols = pl.ds(pl.multiple_of(b * LANES, LANES), LANES)
-        search_ref[:, cols] = as_row(b)
-        model_ref[:, cols] = m_ref[:, cols] + alpha * grow[:, cols]
-        return c
-
-    lax.fori_loop(0, blocks, next_row, 0)
+    model_ref[...] = m_ref[...] + alpha * grow[...]
     bulk_wait(gn, n - 1, recv_sem, 5)
     beta = total(gn)[:, :1] / gamma
     search_ref[...] = search_ref[...] + beta * grow[...]
 
     bulk_wait(st_all, n_sta - 1, send_sem, 0)
-    for which, buf in ((1, rs1), (2, ag1), (3, rs2), (4, ag2), (5, gn)):
+    for which, buf in ((1, rs1), (2, gm), (3, rs2), (5, gn)):
         bulk_wait(buf, n - 1, send_sem, which)
 
 
@@ -336,6 +329,8 @@
     sizes = (n_sta, n_cell, cells, width, piece, scale, mb)
     vmem = pl.BlockSpec(memory_space=pltpu.VMEM)
     wide = pltpu.VMEM((groups, 8, LANES), F32)
+    whole = pltpu.VMEM((n, n_sta, 1, width), F32)
+    line = pltpu.VMEM((n_sta, 1, width), F32)
     message = pltpu.VMEM((n, 1, LANES), F32)
     model_next, residual, search = pl.pallas_call(
         functools.partial(kernel, sizes),
@@ -351,7 +346,7 @@
             pltpu.VMEM((n_sta, 8, width), F32),
             pltpu.VMEM((n_sta, 8, width), F32),
             pltpu.VMEM((n_sta, 8, width), F32),
-            message, message, message, message, message, message, message,
+            whole, whole, line, line, message, message, line, line,
             pltpu.SemaphoreType.DMA((6,)),
             pltpu.SemaphoreType.DMA((6,)),
         ],

time: 79.8 us -> 68.6 us (0.86)
  Pallas kernels: 71.5 us -> 60.3 us
    pallas_call x1, Pallas kernels: 71.5 us -> 60.3 us  [per_device(): pl.pallas_call(functools.partial(kernel, sizes), out_shape=(jax.ShapeDtyp...]
where the time goes in v1:
time: 68.6 us; the launch traced here: 68.3 us
  Pallas kernels  60.3 us (88%)
  local copies, waits for them, and re-layouts  7.33 us (11%)
    pallas_call x1, Pallas kernels, per_device(): pl.pallas_call(functools.partial(kernel, sizes), out_shape=(jax.ShapeDtyp...  60.3 us
    unnamed x12, local copies, waits for them, and re-layouts  3.7 us

profile of v1, /device:TPU:0, one launch (start us, length us, event | category | flops | bytes accessed | tf_op | source)
XLA Modules:
  0.0 68.3 jit_solution(6582320869115996230)
XLA Ops:
  0.6 0.0 copy-start
  0.7 1.0 %copy-done = f32[3,32768]{1,0:T(4,128)S(1)} copy-done((f32[3,32768]{1,0:T(4,128)S(1)}, f32[3,32768]{1,0:T(4,128)}, u32[]{:S(2)}) %copy-start) | copy-done | bytes 393240
  1.7 0.7 pad.13.cell_ref
  2.4 0.0 copy-start.2
  2.4 1.3 %dynamic_slice.7 = f32[4096]{0:T(1024)} dynamic-slice(f32[32768]{0:T(1024)} %param.7, s32[]{:T(128)S(6)} %select_n.4), dynamic_slice_sizes={4096} | dynamic-slice | bytes 32772 | tf_op jit(solution)/shard_map/dynamic_slice | solution.py:324
  3.7 0.0 copy-done.2
  3.7 0.0 copy-start.3
  3.7 0.6 pad.12.st_ref
  4.3 0.1 copy-done.3
  4.4 0.5 pad_bitcast_fusion.data_ref
  4.9 60.3 %shard_map.76 = (f32[1,4096]{1,0:T(1,128)}, f32[1,128]{1,0:T(1,128)}, f32[1,4096]{1,0:T(1,128)}) custom-call(f32[8,256]{1,0:T(8,128)} %pad.12.st_ref, f32[8,4096]{1,0:T(8,128)} %pad.13.cell_ref, f32[1,4096]{1,0:T(1,128)} %bitcast.8, f32[1,4096]{1,0:T(1,128)} %bitcast.11, f32[1,128]{1,0:T(1,128)} %pad_bitcast_fusion.data_ref), custom_call_target="tpu_custom_call" | custom-call | tf_op jit(solution)/shard_map/pallas_call | solution.py:335
  65.2 0.0 copy-start.4
  65.2 0.7 copy-done.4
  65.8 0.5 slice_bitcast_fusion
  66.3 0.0 copy-start.1
  66.3 1.3 %copy.10 = f32[4096]{0:T(1024)} copy(f32[4096]{0:T(1024)} %bitcast.10) | data formatting | bytes 32768
  67.7 0.0 copy-done.1
  67.7 0.6 copy.11
  (1 shorter events, 0.0 us)
Async XLA Ops:
  0.6 1.0 %copy-start = (f32[3,32768]{1,0:T(4,128)S(1)}, f32[3,32768]{1,0:T(4,128)}, u32[]{:S(2)}) copy-start(f32[3,32768]{1,0:T(4,128)} %param.6) | copy-start | bytes 1179652
  2.4 1.3 %copy-start.2 = (f32[3,256]{1,0:T(4,128)S(1)}, f32[3,256]{1,0:T(4,128)}, u32[]{:S(2)}) copy-start(f32[3,256]{1,0:T(4,128)} %param.5) | copy-start | bytes 9220
  3.7 0.7 copy-start.3
  65.2 0.7 copy-start.4
  66.3 1.3 %copy-start.1 = (f32[1,4096]{1,0:T(1,128)S(1)}, f32[1,4096]{1,0:T(1,128)}, u32[]{:S(2)}) copy-start(f32[1,4096]{1,0:T(1,128)} %get-tuple-element.8) | copy-start | bytes 49156
